TPU v7x, 32 devices: a whole 2x2x4 slice. The times are simulated.
32 devices in a mesh: row: 4 (over z), col: 4 (over x, core), rep: 2 (over y).
Axes of the slice: x: 2, y: 2, z: 4, core: 2. Of those that a mesh axis runs over, the one named last changes fastest.
Arguments:
- a_blocks: bfloat16 [8192, 1024], P('row', 'col'), may hold values from -6 to 6
- a_mask: int32 [32, 4], P('row', 'col'), may hold values from 0 to 1, as said below
- b_blocks: bfloat16 [1024, 2048], P('row', 'col'), may hold values from -0.1875 to 0.1875
- b_mask: int32 [4, 8], P('row', 'col'), may hold values from 0 to 1
Outputs:
- c_product: bfloat16 [8192, 2048], P('row', ('col', 'rep'))
Inputs may be any that keep to these rules, and one draw needn't show every extreme that they name: a_mask holds 0 or 1; within each aligned tile of 8 block rows by 1 inner blocks (one device's tile) at most 2 entries are 1, and some tile holds exactly 2.
All inputs are finite; a program needn't handle non-finite values.
Results may differ from a plain program's by a relative error of at most 0.007.
Values may be sent and summed in bfloat16 or wider, within the bound.
No kernel may reach another device: no remote copies, remote signals or barrier semaphores. Data moves between devices by JAX's collectives and lax.ppermute only.
A program may use at most 64 MiB of HBM per device.

v0:
```python
import jax
import jax.numpy as jnp
from jax import lax
from jax.sharding import PartitionSpec as P

BS = 256


def expand(values, pattern):
    block_rows = pattern.shape[0]
    block_cols = pattern.shape[1]
    shaped = values.reshape(block_rows, BS, block_cols, BS) * pattern[:, None, :, None].astype(
        jnp.bfloat16
    )
    return shaped.reshape(block_rows * BS, block_cols * BS)


def pack_blocks(a_blocks, a_mask):
    block_rows = a_mask.shape[0]
    block_cols = a_mask.shape[1]
    slot_count = max(block_rows // 4, 1)
    flat_mask = a_mask.reshape(-1)
    slot_of = jnp.cumsum(flat_mask) - 1
    slot_ids = jnp.arange(slot_count, dtype=jnp.int32)[:, None]
    chosen = (flat_mask[None, :] == 1) & (slot_of[None, :] == slot_ids)
    flat_blocks = (
        a_blocks.reshape(block_rows, BS, block_cols, BS)
        .transpose(0, 2, 1, 3)
        .reshape(block_rows * block_cols, BS * BS)
    )
    packed = jnp.dot(
        chosen.astype(jnp.bfloat16), flat_blocks, preferred_element_type=jnp.float32
    ).astype(jnp.bfloat16)
    positions = jnp.arange(block_rows * block_cols, dtype=jnp.int32)
    chosen_int = chosen.astype(jnp.int32)
    used = jnp.sum(chosen_int, axis=1) > 0
    block_row = jnp.where(
        used, jnp.sum(chosen_int * (positions // block_cols)[None, :], axis=1), block_rows
    )
    block_inner = jnp.where(
        used, jnp.sum(chosen_int * (positions % block_cols)[None, :], axis=1), 0
    )
    codes = jnp.stack([block_row, block_inner], axis=1)
    return (packed.reshape(slot_count, BS, BS), codes)


def per_device(a_blocks, a_mask, b_blocks, b_mask):
    masked_b = expand(b_blocks, b_mask)
    layer_index = lax.axis_index("rep")
    c_width = masked_b.shape[1]
    own_width = c_width // 2
    own_b = lax.dynamic_slice_in_dim(masked_b, layer_index * own_width, own_width, 1)
    column_b = lax.all_gather(own_b, "row", axis=0, tiled=True)
    row_count = a_blocks.shape[0]
    block_rows = a_mask.shape[0]
    inner_local = a_mask.shape[1]
    inner_total = column_b.shape[0] // BS
    stacked_b = column_b.reshape(inner_total, BS, own_width)
    packed, codes = pack_blocks(a_blocks, a_mask)
    slot_count = packed.shape[0]
    row_ids = jnp.arange(block_rows, dtype=jnp.int32)
    blocks = lax.all_gather(packed, "col", axis=0, tiled=True)
    block_codes = lax.all_gather(codes, "col", axis=0, tiled=True)
    item_count = blocks.shape[0]
    owner = jnp.arange(item_count, dtype=jnp.int32) // slot_count
    inner = (owner * inner_local + block_codes[:, 1]).astype(jnp.int32)
    picked = jnp.take(stacked_b, inner, axis=0)
    partial_blocks = jnp.einsum("sij,sjn->sin", blocks, picked, preferred_element_type=jnp.float32)
    selector = (block_codes[:, 0][:, None] == row_ids[None, :]).astype(jnp.float32)
    summed = jnp.einsum("sr,sin->rin", selector, partial_blocks)
    product = summed.reshape(row_count, own_width)
    return product.astype(jnp.bfloat16)


def solution(mesh):
    in_specs = (P("row", "col"), P("row", "col"), P("row", "col"), P("row", "col"))
    out_specs = P("row", ("col", "rep"))
    return jax.shard_map(
        per_device, mesh=mesh, in_specs=in_specs, out_specs=out_specs, check_vma=False
    )
```

profile of v0, /device:TPU:0, one launch (start us, length us, event | category | flops | bytes accessed | tf_op | source)
XLA Modules:
  0.0 45.7 jit_solution(4429056214667428201)
XLA Ops:
  6.5 0.0 copy-start.1
  6.5 0.0 all-gather.3.cloned.1.call-start
  6.5 0.7 %compare_bitcast_fusion = pred[8]{0:T(512)(128)(4,1)S(1)} fusion(s32[8,1]{0,1:T(1,128)} %param.5), kind=kLoop, calls=%fused_computation.20 | loop fusion | flops 8 | bytes 40 | tf_op jit(solution)/shard_map/eq | solution.py:25
  7.3 0.0 copy-done.1
  7.3 0.2 reduce-window.8
  7.5 1.7 %reshape_transpose_reshape.3 = bf16[8,65536]{1,0:T(8,128)(2,1)S(1)} reshape(bf16[2048,256]{1,0:T(8,128)(2,1)} %param.4) | data formatting | bytes 2097152 | tf_op jit(solution)/shard_map/reshape;transpose;reshape | solution.py:29
  9.2 0.1 convert_reduce_fusion
  9.3 0.4 convolution_convert_fusion
  9.7 0.7 %copy.29 = bf16[1,2,256,256]{3,2,1,0:T(8,128)(2,1)} copy(bf16[1,2,256,256]{3,1,2,0:T(2,128)(2,1)S(1)} %bitcast.31) | data formatting | bytes 524288
  10.5 0.0 copy-start
  10.5 0.0 all-gather.3.cloned.1.call-update
  10.5 0.1 copy.21
  10.6 6.0 %all-gather = s32[4,2,2]{2,1,0:T(2,128)S(1)} all-gather(s32[1,2,2]{2,1,0:T(2,128)S(1)} %pad_bitcast_fusion), channel_id=1, replica_groups=mesh['row'=4,'col'=4,'rep'=2] {'col'}, dimensions={0}, use_global_device_ids=true | all-gather | bytes 80 | tf_op jit(solution)/shard_map/all_gather | solution.py:63
  16.6 0.0 copy-start.2
  16.6 0.7 %copy-done.2 = s32[1,2]{1,0:T(1,128)S(1)} copy-done((s32[1,2]{1,0:T(1,128)S(1)}, s32[1,2]{1,0:T(1,128)}, u32[]{:S(2)}) %copy-start.2) | copy-done | bytes 32
  17.3 0.1 broadcast_bitcast_fusion
  17.4 0.1 fusion.15
  17.4 0.1 copy.19
  17.5 0.1 copy.20
  17.6 0.1 dynamic-slice
  17.7 0.0 copy-done
  17.8 16.9 %all_gather.11 = bf16[1024,256]{1,0:T(8,128)(2,1)S(1)} all-gather(bf16[256,256]{1,0:T(8,128)(2,1)S(1)} %dynamic-slice_multiply_fusion), channel_id=1, replica_groups=mesh['row'=4,'col'=4,'rep'=2] {'row'}, dimensions={0}, use_global_device_ids=true | all-gather | bytes 655360 | tf_op jit(solution)/shard_map/all_gather | solution.py:53
  34.6 0.6 %gather_fusion = bf16[8,256,256]{2,1,0:T(8,128)(2,1)S(1)} fusion(bf16[4,256,256]{2,1,0:T(8,128)(2,1)S(1)} %bitcast.30, s32[1024]{0:T(1024)S(1)} %pad_clamp_fusion), kind=kCustom, calls=%fused_computation | custom fusion | bytes 2097184 | tf_op jit(solution)/shard_map/jit(_take)/gather | solution.py:67
  35.2 0.0 all-gather.3.cloned.1.call-done
  35.3 1.7 %fusion.5 = bf16[8,256,256]{2,1,0:T(8,128)(2,1)S(1)} fusion(bf16[8,256,256]{2,1,0:T(8,128)(2,1)} %all-gather.3.cloned.1.call-done, bf16[8,256,256]{2,1,0:T(8,128)(2,1)S(1)} %gather_fusion, pred[8]{0:T(512)(128)(4,1)S(1)} %get-tuple-element.7), kind=kOutput, calls=%fused_computation.5 | convolution fusion | flops 268959744 | bytes 3145736 | tf_op jit(solution)/shard_map/sij,sjn->sin/dot_general | solution.py:68
  37.0 0.7 %fusion.2 = bf16[8,256,256]{2,0,1:T(8,128)(2,1)S(1)} fusion(bf16[8,256,256]{2,1,0:T(8,128)(2,1)S(1)} %fusion.5, s32[8]{0:T(128)S(1)} %bitcast.34), kind=kOutput, calls=%fused_computation.4 | convolution fusion | flops 8388672 | bytes 2097184 | tf_op jit(solution)/shard_map/sr,sin->rin/dot_general | solution.py:70
  37.7 1.2 %copy.17 = bf16[8,256,256]{2,1,0:T(8,128)(2,1)} copy(bf16[8,256,256]{2,0,1:T(8,128)(2,1)S(1)} %fusion.2) | data formatting | bytes 2097152 | tf_op jit(solution)/shard_map/convert_element_type | solution.py:72
  (8 shorter events, 0.1 us)
Async XLA Ops:
  6.5 0.7 %copy-start.1 = (s32[8,1]{0,1:T(1,128)S(1)}, s32[8,1]{0,1:T(1,128)}, u32[]{:S(2)}) copy-start(s32[8,1]{0,1:T(1,128)} %param.5) | copy-start | bytes 100
  6.5 28.7 %all-gather.3.cloned.1.call-start = ((), (), s32[]{:S(2)}) async-start(), calls=%async_computation | async-start | bytes 1310720 | tf_op jit(solution)/shard_map/all_gather | solution.py:62
  10.5 7.2 %copy-start = (bf16[256,512]{1,0:T(8,128)(2,1)S(1)}, bf16[256,512]{1,0:T(8,128)(2,1)}, u32[]{:S(2)}) copy-start(bf16[256,512]{1,0:T(8,128)(2,1)} %param.6) | copy-start | bytes 786436
  16.6 0.7 %copy-start.2 = (s32[1,2]{1,0:T(1,128)S(1)}, s32[1,2]{1,0:T(1,128)}, u32[]{:S(2)}) copy-start(s32[1,2]{1,0:T(1,128)} %param.7) | copy-start | bytes 28
Sparse Core Ops, SparseCore 0:
  10.6 19.4 all-gather.2
where the time goes:
time: 46 us; the launch traced here: 45.7 us
  blocking collectives  22.9 us (50%)
  between operations  13.5 us (29%)
  local copies, waits for them, and re-layouts  5.38 us (12%)
  matrix products  2.86 us (6%)
  other arithmetic  1.12 us (2%)
    all_gather x1, blocking collectives, per_device(): column_b = lax.all_gather(own_b, 'row', axis=0, tiled=True)  16.9 us
    all_gather x1, blocking collectives, per_device(): block_codes = lax.all_gather(codes, 'col', axis=0, tiled=True)  6 us
    dot_general x1, matrix products, per_device(): jnp.einsum('sij,sjn->sin', blocks, picked, preferred_element_type=jnp.flo...  1.74 us
    unnamed x13, local copies, waits for them, and re-layouts  1.74 us
    another operation x1, local copies, waits for them, and re-layouts, pack_blocks(): flat_blocks = a_blocks.reshape(block_rows, BS, block_cols, BS).transpose(...  1.7 us
    convert_element_type x1, local copies, waits for them, and re-layouts, per_device(): return product.astype(jnp.bfloat16)  1.18 us
  transfers between devices with their start and end apart: 1, of which 0 were waited for; matrix products, arithmetic and copies ran while one was open for 3% of the time, Pallas kernels for 0%

commit v1 on v0

v1 whole, which is shorter than its diff:
```python
import functools

import jax
import jax.numpy as jnp
from jax import lax
from jax.experimental import pallas as pl
from jax.experimental.pallas import tpu as pltpu
from jax.sharding import PartitionSpec as P


BS = 256
CODE_ALIGN = 16


def pack_kernel(slots, mask_ref, a_ref, out_ref, sem):
    rows, cols = mask_ref.shape
    cells = rows * cols
    place = [jnp.int32(cells)] * slots
    count = jnp.int32(0)
    for cell in range(cells):
        hit = mask_ref[cell // cols, cell % cols] == 1
        for slot in range(slots):
            place[slot] = jnp.where(hit & (count == slot), cell, place[slot])
        count = count + hit.astype(jnp.int32)
    copies = []
    for slot in range(slots):
        cell = jnp.minimum(place[slot], cells - 1)
        copies.append(
            pltpu.make_async_copy(
                a_ref.at[pl.ds((cell // cols) * BS, BS), pl.ds((cell % cols) * BS, BS)]
                if cols > 1
                else a_ref.at[pl.ds(cell * BS, BS), :],
                out_ref.at[pl.ds(slot * BS, BS), :],
                sem.at[slot],
            )
        )
        copies[-1].start()
    code_rows = out_ref.shape[0] - slots * BS
    index = lax.broadcasted_iota(jnp.int32, (code_rows, BS), 0)
    codes = jnp.full((code_rows, BS), cells, jnp.int32)
    for slot in range(slots):
        codes = jnp.where(index == slot, place[slot], codes)
    out_ref[pl.ds(slots * BS, code_rows), :] = codes.astype(jnp.float32).astype(jnp.bfloat16)
    for copy in copies:
        copy.wait()


def product_kernel(slots, inner_local, b_blocks, *refs):
    owner_ref = refs[0]
    rest = refs[1:]
    out_ref, total, stacked = rest[-3:]
    rest = rest[:-3]
    n_b = b_blocks
    a_refs, b_refs = rest[: len(rest) - n_b], rest[len(rest) - n_b :]
    rows = out_ref.shape[0]
    n_a = len(a_refs)
    cells = (rows // BS) * inner_local
    total[...] = jnp.zeros_like(total)
    depth = b_refs[0].shape[0]
    for i, b_ref in enumerate(b_refs):
        stacked[pl.ds(pl.multiple_of(owner_ref[n_a + i] * depth, depth), depth), :] = b_ref[...]
    for i, a_ref in enumerate(a_refs):
        code_rows = a_ref.shape[0] - slots * BS
        codes = a_ref[pl.ds(slots * BS, code_rows), :].astype(jnp.float32)
        index = lax.broadcasted_iota(jnp.int32, codes.shape, 0)
        for slot in range(slots):
            code = jnp.max(jnp.where(index == slot, codes, 0.0)).astype(jnp.int32)
            used = code < cells
            row = jnp.where(used, code // inner_local, rows // BS)
            inner = jnp.where(used, code % inner_local, 0) + owner_ref[i] * inner_local
            where = pl.ds(pl.multiple_of(row * BS, BS), BS)
            total[where, :] += jnp.dot(
                a_ref[pl.ds(slot * BS, BS), :],
                stacked[pl.ds(pl.multiple_of(inner * BS, BS), BS), :],
                preferred_element_type=jnp.float32,
            )
    out_ref[...] = total[pl.ds(0, rows), :].astype(jnp.bfloat16)


def exchange(values, axis, n):
    me = lax.axis_index(axis)
    held = [(values, me)]
    if n & (n - 1):
        for step in range(1, n):
            moved = lax.ppermute(values, axis, [(i, (i + step) % n) for i in range(n)])
            held.append((moved, lax.rem(me + n - step, n)))
        return held
    step = n // 2
    while step:
        pairs = [(i, i ^ step) for i in range(n)]
        held += [(lax.ppermute(v, axis, pairs), owner ^ step) for v, owner in held]
        step //= 2
    return held


def per_device(shape, a_blocks, a_mask, b_blocks, b_mask):
    own_width = b_blocks.shape[1] // shape["rep"]
    layer = lax.axis_index("rep")
    depth = b_blocks.shape[0]
    own_b = lax.dynamic_slice_in_dim(b_blocks, layer * own_width, own_width, 1)
    column_mask = jnp.repeat(b_mask, BS, axis=1)
    own_mask = lax.dynamic_slice_in_dim(column_mask, layer * own_width, own_width, 1)
    own_mask = jnp.repeat(own_mask, BS, axis=0).astype(jnp.bfloat16)
    own_b = own_b * own_mask
    row_n, col_n = shape["row"], shape["col"]
    me_row = lax.axis_index("row")
    b_held = [(own_b, me_row)]
    for step in range(1, row_n):
        moved = lax.ppermute(own_b, "row", [(i, (i + step) % row_n) for i in range(row_n)])
        b_held.append((moved, lax.rem(me_row + row_n - step, row_n)))

    rows = a_blocks.shape[0]
    block_rows, inner_local = a_mask.shape
    slots = max(block_rows // 4, 1)
    code_rows = -(-slots // CODE_ALIGN) * CODE_ALIGN
    packed = pl.pallas_call(
        functools.partial(pack_kernel, slots),
        out_shape=jax.ShapeDtypeStruct((slots * BS + code_rows, BS), jnp.bfloat16),
        in_specs=[
            pl.BlockSpec(memory_space=pltpu.SMEM),
            pl.BlockSpec(memory_space=pl.ANY),
        ],
        out_specs=pl.BlockSpec(memory_space=pltpu.VMEM),
        scratch_shapes=[pltpu.SemaphoreType.DMA((slots,))],
        compiler_params=pltpu.CompilerParams(vmem_limit_bytes=4 << 20),
        name="pack",
    )(a_mask, a_blocks)
    a_held = exchange(packed, "col", col_n)

    owners = jnp.stack([o for _, o in a_held] + [o for _, o in b_held]).astype(jnp.int32)
    return pl.pallas_call(
        functools.partial(product_kernel, slots, inner_local, row_n),
        out_shape=jax.ShapeDtypeStruct((rows, own_width), jnp.bfloat16),
        in_specs=[pl.BlockSpec(memory_space=pltpu.SMEM)]
        + [pl.BlockSpec(memory_space=pltpu.VMEM)] * (col_n + row_n),
        out_specs=pl.BlockSpec(memory_space=pltpu.VMEM),
        scratch_shapes=[
            pltpu.VMEM((rows + BS, own_width), jnp.float32),
            pltpu.VMEM((row_n * depth, own_width), jnp.bfloat16),
        ],
        compiler_params=pltpu.CompilerParams(vmem_limit_bytes=16 << 20),
        name="product",
    )(owners, *[v for v, _ in a_held], *[v for v, _ in b_held])


def solution(mesh):
    in_specs = (P("row", "col"), P("row", "col"), P("row", "col"), P("row", "col"))
    out_specs = P("row", ("col", "rep"))
    return jax.shard_map(
        functools.partial(per_device, dict(mesh.shape)),
        mesh=mesh,
        in_specs=in_specs,
        out_specs=out_specs,
        check_vma=False,
    )
```

time: 46 us -> 31.7 us (0.69)
  blocking collectives: 22.9 us -> 0 us
  waiting for transfers between devices: 0.04 us -> 18 us
  between operations: 13.5 us -> 0.03 us
  starting transfers between devices: 0.01 us -> 8.03 us
  Pallas kernels: 0 us -> 3.26 us
  local copies, waits for them, and re-layouts: 5.38 us -> 2.13 us
  matrix products: 2.86 us -> 0 us
  other arithmetic: 1.12 us -> 0.11 us
    all_gather x2 -> x0, blocking collectives: 22.9 us -> none  [the longest x1 16.9 us: per_device(): column_b = lax.all_gather(own_b, 'row', axis=0, tiled=True)]
    ppermute x0 -> x6, waiting for transfers between devices: none -> 18 us  [the longest x3 11 us: per_device(): lax.ppermute(own_b, 'row', [(i, (i + step) % row_n) for i in range(row_n)])]
    ppermute x0 -> x6, starting transfers between devices: none -> 8.03 us  [the longest x3 4.92 us: per_device(): lax.ppermute(own_b, 'row', [(i, (i + step) % row_n) for i in range(row_n)])]
    pallas_call x0 -> x2, Pallas kernels: none -> 3.26 us  [the longest x1 2.27 us: per_device(): pl.pallas_call(functools.partial(product_kernel, slots, inner_local, row_...]
    dot_general x3 -> x0, matrix products: 2.86 us -> none  [the longest x1 1.74 us: per_device(): jnp.einsum('sij,sjn->sin', blocks, picked, preferred_element_type=jnp.flo...]
    another operation x1, local copies, waits for them, and re-layouts: 1.7 us -> 0.08 us  [per_device(): jnp.stack([o for _, o in a_held] + [o for _, o in b_held]).astype(jnp.int32)]
    convert_element_type x1 -> x0, local copies, waits for them, and re-layouts: 1.18 us -> none  [per_device(): return product.astype(jnp.bfloat16)]
    eq x1 -> x0, other arithmetic: 0.73 us -> none  [pack_blocks(): chosen = (flat_mask[None, :] == 1) & (slot_of[None, :] == slot_ids)]
  transfers between devices with their start and end apart: 1 -> 6, of which waited for: 0 -> 3; matrix products, arithmetic and copies ran while one was open for 3% -> 1% of each run, Pallas kernels for 0% -> 0%
where the time goes in v1:
time: 31.7 us; the launch traced here: 31.5 us
  waiting for transfers between devices  18 us (57%)
  starting transfers between devices  8.03 us (25%)
  Pallas kernels  3.26 us (10%)
  local copies, waits for them, and re-layouts  2.13 us (7%)
    ppermute x3, waiting for transfers between devices, per_device(): lax.ppermute(own_b, 'row', [(i, (i + step) % row_n) for i in range(row_n)])  11 us
    ppermute x3, waiting for transfers between devices, exchange(): held += [(lax.ppermute(v, axis, pairs), owner ^ step) for v, owner in held]  6.92 us
    ppermute x3, starting transfers between devices, per_device(): lax.ppermute(own_b, 'row', [(i, (i + step) % row_n) for i in range(row_n)])  4.92 us
    ppermute x3, starting transfers between devices, exchange(): held += [(lax.ppermute(v, axis, pairs), owner ^ step) for v, owner in held]  3.11 us
    pallas_call x1, Pallas kernels, per_device(): pl.pallas_call(functools.partial(product_kernel, slots, inner_local, row_...  2.27 us
    unnamed x9, local copies, waits for them, and re-layouts  2.05 us
    pallas_call x1, Pallas kernels, per_device(): pl.pallas_call(functools.partial(pack_kernel, slots), out_shape=jax.Shape...  0.99 us
  transfers between devices with their start and end apart: 6, of which 3 were waited for; matrix products, arithmetic and copies ran while one was open for 1% of the time, Pallas kernels for 0%

profile of v1, /device:TPU:0, one launch (start us, length us, event | category | flops | bytes accessed | tf_op | source)
XLA Modules:
  0.0 31.5 jit_solution(11084181924802233061)
XLA Ops:
  0.0 0.0 copy-start
  0.0 0.7 %copy.5.mask_ref = s32[8,1]{1,0:T(8,128)S(1)} copy(s32[8,1]{0,1:T(1,128)} %param.5) | data formatting | bytes 64 | tf_op args[1]
  0.7 0.0 copy-start.1
  0.7 1.2 %copy-done.1 = bf16[2048,256]{1,0:T(8,128)(2,1)S(1)} copy-done((bf16[2048,256]{1,0:T(8,128)(2,1)S(1)}, bf16[2048,256]{1,0:T(8,128)(2,1)}, u32[]{:S(2)}) %copy-start.1) | copy-done | bytes 1048600
  2.0 0.0 copy-start.2
  2.0 1.0 %pack.1.refs_1_ = bf16[528,256]{1,0:T(8,128)(2,1)S(1)} custom-call(s32[8,1]{1,0:T(8,128)S(1)} %copy.5.mask_ref, bf16[2048,256]{1,0:T(8,128)(2,1)S(1)} %copy-done.1), custom_call_target="tpu_custom_call" | custom-call | tf_op jit(solution)/shard_map/pack/pallas_call | solution.py:116
  3.0 0.6 %collective-permute-start.1 = (bf16[528,256]{1,0:T(8,128)(2,1)S(1)}, bf16[528,256]{1,0:T(8,128)(2,1)S(1)}, u32[]{:S(2)}, u32[]{:S(2)}) collective-permute-start(bf16[528,256]{1,0:T(8,128)(2,1)S(1)} %pack.1.refs_1_), channel_id=1, source_target_pairs={{0,2},{2,0},{4,6},{6,4},{1,3},{3,1},{5,7},{7,5},{8,10},{10,8},{12,... | collective-permute-start | bytes 811016 | tf_op jit(solution)/shard_map/ppermute | solution.py:91
  3.5 2.6 %collective-permute-start = (bf16[528,256]{1,0:T(8,128)(2,1)S(1)}, bf16[528,256]{1,0:T(8,128)(2,1)S(1)}, u32[]{:S(2)}, u32[]{:S(2)}) collective-permute-start(bf16[528,256]{1,0:T(8,128)(2,1)S(1)} %pack.1.refs_1_), channel_id=1, source_target_pairs={{0,4},{2,6},{4,0},{6,2},{1,5},{3,7},{5,1},{7,3},{8,12},{10,14},{12... | collective-permute-start | bytes 811016 | tf_op jit(solution)/shard_map/ppermute | solution.py:91
  6.1 0.0 copy-done
  6.1 0.1 broadcast_bitcast_fusion
  6.2 0.1 dynamic-slice_convert_fusion
  6.2 6.9 %collective-permute-done.refs_2_ = bf16[528,256]{1,0:T(8,128)(2,1)S(1)} collective-permute-done((bf16[528,256]{1,0:T(8,128)(2,1)S(1)}, bf16[528,256]{1,0:T(8,128)(2,1)S(1)}, u32[]{:S(2)}, u32[]{:S(2)}) %collective-permute-start) | collective-permute-done | bytes 270368 | tf_op jit(solution)/shard_map/ppermute | solution.py:91
  13.2 0.0 collective-permute-start.2
  13.2 0.0 copy-done.2
  13.2 3.9 %collective-permute-start.5 = (bf16[256,256]{1,0:T(8,128)(2,1)S(1)}, bf16[256,256]{1,0:T(8,128)(2,1)S(1)}, u32[]{:S(2)}, u32[]{:S(2)}) collective-permute-start(bf16[256,256]{1,0:T(8,128)(2,1)S(1)} %dynamic-slice_multiply_fusion.refs_5_), channel_id=1, source_target_pairs={{0,24},{8,0},{16,8},{24,16},{1,25},{9,1},{17,9},{25,17},{2,26},{10... | collective-permute-start | bytes 393224 | tf_op jit(solution)/shard_map/ppermute | solution.py:109
  17.1 0.0 collective-permute-start.4
  17.1 1.0 %collective-permute-start.3 = (bf16[256,256]{1,0:T(8,128)(2,1)S(1)}, bf16[256,256]{1,0:T(8,128)(2,1)S(1)}, u32[]{:S(2)}, u32[]{:S(2)}) collective-permute-start(bf16[256,256]{1,0:T(8,128)(2,1)S(1)} %dynamic-slice_multiply_fusion.refs_5_), channel_id=1, source_target_pairs={{0,8},{8,16},{16,24},{24,0},{1,9},{9,17},{17,25},{25,1},{2,10},{10... | collective-permute-start | bytes 393224 | tf_op jit(solution)/shard_map/ppermute | solution.py:109
  18.1 0.1 stack.35.refs_0_
  18.2 2.9 %collective-permute-done.5.refs_8_ = bf16[256,256]{1,0:T(8,128)(2,1)S(1)} collective-permute-done((bf16[256,256]{1,0:T(8,128)(2,1)S(1)}, bf16[256,256]{1,0:T(8,128)(2,1)S(1)}, u32[]{:S(2)}, u32[]{:S(2)}) %collective-permute-start.5) | collective-permute-done | bytes 131104 | tf_op jit(solution)/shard_map/ppermute | solution.py:109
  21.1 8.2 %collective-permute-done.4.refs_7_ = bf16[256,256]{1,0:T(8,128)(2,1)S(1)} collective-permute-done((bf16[256,256]{1,0:T(8,128)(2,1)S(1)}, bf16[256,256]{1,0:T(8,128)(2,1)S(1)}, u32[]{:S(2)}, u32[]{:S(2)}) %collective-permute-start.4) | collective-permute-done | bytes 131104 | tf_op jit(solution)/shard_map/ppermute | solution.py:109
  29.2 0.0 collective-permute-done.3.refs_6_
  29.3 0.0 collective-permute-done.1.refs_3_
  29.3 0.0 collective-permute-done.2.refs_4_
  29.3 2.3 %product.1 = bf16[2048,256]{1,0:T(8,128)(2,1)} custom-call(s32[8]{0:T(128)S(1)} %stack.35.refs_0_, bf16[528,256]{1,0:T(8,128)(2,1)S(1)} %pack.1.refs_1_, bf16[528,256]{1,0:T(8,128)(2,1)S(1)} %collective-permute-done.refs_2_, bf16[528,256]{1,0:T(8,128)(2,1)S(1)} %collective-permute-done.1.refs_3_, bf16[528,256]{1,0:T(8,128)(2,1)S(1)} %collective-permute-done.2.refs_4_, ...), custom_call_target="tpu_custom_call" | custom-call | tf_op jit(solution)/shard_map/product/pallas_call | solution.py:131
  (2 shorter events, 0.0 us)
Async XLA Ops:
  0.0 6.1 %copy-start = (s32[1,2]{1,0:T(1,128)S(1)}, s32[1,2]{1,0:T(1,128)}, u32[]{:S(2)}) copy-start(s32[1,2]{1,0:T(1,128)} %param.7) | copy-start | bytes 28
  0.7 1.2 %copy-start.1 = (bf16[2048,256]{1,0:T(8,128)(2,1)S(1)}, bf16[2048,256]{1,0:T(8,128)(2,1)}, u32[]{:S(2)}) copy-start(bf16[2048,256]{1,0:T(8,128)(2,1)} %a_ref.1) | copy-start | bytes 3145732
  2.0 11.2 %copy-start.2 = (bf16[256,512]{1,0:T(8,128)(2,1)S(1)}, bf16[256,512]{1,0:T(8,128)(2,1)}, u32[]{:S(2)}) copy-start(bf16[256,512]{1,0:T(8,128)(2,1)} %param.6) | copy-start | bytes 786436
  3.0 26.3 %collective-permute-start.1 = (bf16[528,256]{1,0:T(8,128)(2,1)S(1)}, bf16[528,256]{1,0:T(8,128)(2,1)S(1)}, u32[]{:S(2)}, u32[]{:S(2)}) collective-permute-start(bf16[528,256]{1,0:T(8,128)(2,1)S(1)} %pack.1.refs_1_), channel_id=1, source_target_pairs={{0,2},{2,0},{4,6},{6,4},{1,3},{3,1},{5,7},{7,5},{8,10},{10,8},{12,... | collective-permute-start | bytes 811016 | tf_op jit(solution)/shard_map/ppermute | solution.py:91
  3.5 9.6 %collective-permute-start = (bf16[528,256]{1,0:T(8,128)(2,1)S(1)}, bf16[528,256]{1,0:T(8,128)(2,1)S(1)}, u32[]{:S(2)}, u32[]{:S(2)}) collective-permute-start(bf16[528,256]{1,0:T(8,128)(2,1)S(1)} %pack.1.refs_1_), channel_id=1, source_target_pairs={{0,4},{2,6},{4,0},{6,2},{1,5},{3,7},{5,1},{7,3},{8,12},{10,14},{12... | collective-permute-start | bytes 811016 | tf_op jit(solution)/shard_map/ppermute | solution.py:91
  13.2 16.1 %collective-permute-start.2 = (bf16[528,256]{1,0:T(8,128)(2,1)S(1)}, bf16[528,256]{1,0:T(8,128)(2,1)S(1)}, u32[]{:S(2)}, u32[]{:S(2)}) collective-permute-start(bf16[528,256]{1,0:T(8,128)(2,1)S(1)} %collective-permute-done.refs_2_), channel_id=1, source_target_pairs={{0,2},{2,0},{4,6},{6,4},{1,3},{3,1},{5,7},{7,5},{8,10},{10,8},{12,... | collective-permute-start | bytes 811016 | tf_op jit(solution)/shard_map/ppermute | solution.py:91
  13.2 7.9 %collective-permute-start.5 = (bf16[256,256]{1,0:T(8,128)(2,1)S(1)}, bf16[256,256]{1,0:T(8,128)(2,1)S(1)}, u32[]{:S(2)}, u32[]{:S(2)}) collective-permute-start(bf16[256,256]{1,0:T(8,128)(2,1)S(1)} %dynamic-slice_multiply_fusion.refs_5_), channel_id=1, source_target_pairs={{0,24},{8,0},{16,8},{24,16},{1,25},{9,1},{17,9},{25,17},{2,26},{10... | collective-permute-start | bytes 393224 | tf_op jit(solution)/shard_map/ppermute | solution.py:109
  17.1 12.1 %collective-permute-start.4 = (bf16[256,256]{1,0:T(8,128)(2,1)S(1)}, bf16[256,256]{1,0:T(8,128)(2,1)S(1)}, u32[]{:S(2)}, u32[]{:S(2)}) collective-permute-start(bf16[256,256]{1,0:T(8,128)(2,1)S(1)} %dynamic-slice_multiply_fusion.refs_5_), channel_id=1, source_target_pairs={{0,16},{8,24},{16,0},{24,8},{1,17},{9,25},{17,1},{25,9},{2,18},{10... | collective-permute-start | bytes 393224 | tf_op jit(solution)/shard_map/ppermute | solution.py:109
  17.1 12.1 %collective-permute-start.3 = (bf16[256,256]{1,0:T(8,128)(2,1)S(1)}, bf16[256,256]{1,0:T(8,128)(2,1)S(1)}, u32[]{:S(2)}, u32[]{:S(2)}) collective-permute-start(bf16[256,256]{1,0:T(8,128)(2,1)S(1)} %dynamic-slice_multiply_fusion.refs_5_), channel_id=1, source_target_pairs={{0,8},{8,16},{16,24},{24,0},{1,9},{9,17},{17,25},{25,1},{2,10},{10... | collective-permute-start | bytes 393224 | tf_op jit(solution)/shard_map/ppermute | solution.py:109

commit v2 on v1

v2 whole, which is shorter than its diff:
```python
import functools

import jax
import jax.numpy as jnp
from jax import lax
from jax.experimental import pallas as pl
from jax.experimental.pallas import tpu as pltpu
from jax.sharding import PartitionSpec as P


BS = 256
CODE_ALIGN = 16


def block(index):
    start = index * BS
    return pl.ds(start if isinstance(index, int) else pl.multiple_of(start, BS), BS)


def prep_kernel(slots, rows, cols, am_ref, a_ref, bm_ref, b_ref, pack_ref, own_ref, am, bm, a_sem, b_sem, m_sem):
    width = own_ref.shape[1]
    wide = width // BS
    layer = lax.axis_index("rep")
    load_am = pltpu.make_async_copy(am_ref, am, m_sem.at[0])
    load_bm = pltpu.make_async_copy(bm_ref, bm, m_sem.at[1])
    load_b = pltpu.make_async_copy(
        b_ref.at[:, pl.ds(pl.multiple_of(layer * width, width), width)], own_ref, b_sem
    )
    load_am.start()
    load_bm.start()
    load_b.start()
    load_am.wait()
    cells = rows * cols
    place = [jnp.int32(cells)] * slots
    count = jnp.int32(0)
    for cell in range(cells):
        hit = am[cell % cols, cell // cols] == 1
        for slot in range(slots):
            place[slot] = jnp.where(hit & (count == slot), cell, place[slot])
        count = count + hit.astype(jnp.int32)
    copies = []
    for slot in range(slots):
        cell = jnp.minimum(place[slot], cells - 1)
        across = block(cell % cols) if cols > 1 else slice(None)
        copies.append(
            pltpu.make_async_copy(
                a_ref.at[block(cell // cols if cols > 1 else cell), across],
                pack_ref.at[block(slot), :],
                a_sem.at[slot],
            )
        )
        copies[-1].start()
    code_rows = pack_ref.shape[0] - slots * BS
    index = lax.broadcasted_iota(jnp.int32, (code_rows, BS), 0)
    codes = jnp.full((code_rows, BS), cells, jnp.int32)
    for slot in range(slots):
        codes = jnp.where(index == slot, place[slot], codes)
    pack_ref[pl.ds(slots * BS, code_rows), :] = codes.astype(jnp.float32).astype(jnp.bfloat16)
    load_bm.wait()
    load_b.wait()
    for down in range(own_ref.shape[0] // BS):
        for over in range(wide):
            keep = bm[down, layer * wide + over].astype(jnp.float32)
            part = (block(down), block(over))
            own_ref[part] = (own_ref[part].astype(jnp.float32) * keep).astype(jnp.bfloat16)
    for copy in copies:
        copy.wait()


def add_products(slots, inner_local, rows, a_refs, a_owners, b_refs, b_owners, total):
    cells = rows // BS * inner_local
    depth = b_refs[0].shape[0] // BS
    found = []
    for a_ref, owner in zip(a_refs, a_owners):
        codes = a_ref[pl.ds(slots * BS, CODE_ALIGN), pl.ds(0, 128)].astype(jnp.float32)
        index = lax.broadcasted_iota(jnp.int32, codes.shape, 0)
        for slot in range(slots):
            code = jnp.max(jnp.where(index == slot, codes, 0.0)).astype(jnp.int32)
            row = code // inner_local if inner_local > 1 else code
            inner = owner * inner_local + (code % inner_local if inner_local > 1 else 0)
            found.append((a_ref, slot, code < cells, row, inner))
    for a_ref, slot, used, row, inner in found:
        for b_ref, owner in zip(b_refs, b_owners):

            @pl.when(used & (inner // depth == owner))
            def _():
                inside = block(inner % depth) if depth > 1 else slice(None)
                where = block(row)
                total[where, :] += jnp.dot(
                    a_ref[block(slot), :], b_ref[inside, :], preferred_element_type=jnp.float32
                )


def early_kernel(slots, inner_local, a_of, b_of, *refs):
    a_refs, b_refs, total = refs[: len(a_of)], refs[len(a_of) : -1], refs[-1]
    total[...] = jnp.zeros_like(total)
    a_owners = [of(lax.axis_index("col")) for of in a_of]
    b_owners = [of(lax.axis_index("row")) for of in b_of]
    add_products(slots, inner_local, total.shape[0], a_refs, a_owners, b_refs, b_owners, total)


def late_kernel(slots, inner_local, a_of, b_of, total_ref, *refs):
    a_refs, b_refs = refs[: len(a_of)], refs[len(a_of) : -4]
    total, out_ref, stage, sem = refs[-4:]
    a_owners = [of(lax.axis_index("col")) for of in a_of]
    b_owners = [of(lax.axis_index("row")) for of in b_of]
    add_products(slots, inner_local, total.shape[0], a_refs, a_owners, b_refs, b_owners, total)
    copies = []
    for row in range(total.shape[0] // BS):
        stage[block(row), :] = total[block(row), :].astype(jnp.bfloat16)
        copies.append(
            pltpu.make_async_copy(stage.at[block(row), :], out_ref.at[block(row), :], sem.at[row])
        )
        copies[-1].start()
    for copy in copies:
        copy.wait()


def flip(step):
    return lambda me: me ^ step


def behind(step, n):
    return lambda me: lax.rem(me + n - step, n)


def hops(n):
    if n & (n - 1):
        return [([(i, (i + s) % n) for i in range(n)], behind(s, n)) for s in range(1, n)]
    order = list(range(n // 2, n)) + list(range(1, n // 2))
    return [([(i, i ^ s) for i in range(n)], flip(s)) for s in order]


def spread(values, axis, n):
    same = lambda me: me
    held = [(values, same)]
    if n & (n - 1):
        return held + [
            (lax.ppermute(values, axis, pairs), of) for pairs, of in hops(n)
        ]
    step = n // 2
    masks = [(values, 0)]
    while step:
        pairs = [(i, i ^ step) for i in range(n)]
        fresh = []
        for v, mask in masks:
            fresh.append((lax.ppermute(v, axis, pairs), mask ^ step))
        masks += fresh
        step //= 2
    return [(v, flip(mask)) for v, mask in masks]


VMEM = pl.BlockSpec(memory_space=pltpu.VMEM)
HBM = pl.BlockSpec(memory_space=pltpu.HBM)


def per_device(shape, a_blocks, a_mask, b_blocks, b_mask):
    row_n, col_n = shape["row"], shape["col"]
    own_width = b_blocks.shape[1] // shape["rep"]
    depth = b_blocks.shape[0]
    rows = a_blocks.shape[0]
    block_rows, inner_local = a_mask.shape
    slots = max(block_rows // 4, 1)
    code_rows = -(-slots // CODE_ALIGN) * CODE_ALIGN
    packed, own_b = pl.pallas_call(
        functools.partial(prep_kernel, slots, block_rows, inner_local),
        out_shape=[
            pltpu.VMEM((slots * BS + code_rows, BS), jnp.bfloat16),
            pltpu.VMEM((depth, own_width), jnp.bfloat16),
        ],
        in_specs=[HBM] * 4,
        out_specs=[VMEM] * 2,
        scratch_shapes=[
            pltpu.SMEM(a_mask.shape[::-1], jnp.int32),
            pltpu.SMEM(b_mask.shape, jnp.int32),
            pltpu.SemaphoreType.DMA((slots,)),
            pltpu.SemaphoreType.DMA,
            pltpu.SemaphoreType.DMA((2,)),
        ],
        compiler_params=pltpu.CompilerParams(vmem_limit_bytes=60 << 20),
        name="prep",
    )(a_mask.T, a_blocks, b_mask, b_blocks)
    b_held = [(own_b, lambda me: me)]
    for pairs, of in hops(row_n):
        b_held.append((lax.ppermute(own_b, "row", pairs), of))
    a_held = spread(packed, "col", col_n)
    far = -(-row_n // 2)
    early, late = b_held[:1] + b_held[1 + far :], b_held[1 : 1 + far]
    a_of = [of for _, of in a_held]
    total = pl.pallas_call(
        functools.partial(early_kernel, slots, inner_local, a_of, [of for _, of in early]),
        out_shape=jax.ShapeDtypeStruct((rows, own_width), jnp.float32),
        in_specs=[VMEM] * (len(a_held) + len(early)),
        out_specs=VMEM,
        compiler_params=pltpu.CompilerParams(vmem_limit_bytes=8 << 20),
        cost_estimate=pl.CostEstimate(flops=1 << 30, bytes_accessed=1 << 22, transcendentals=0),
        name="early",
    )(*[v for v, _ in a_held], *[v for v, _ in early])
    _, product = pl.pallas_call(
        functools.partial(late_kernel, slots, inner_local, a_of, [of for _, of in late]),
        out_shape=[
            jax.ShapeDtypeStruct((rows, own_width), jnp.float32),
            jax.ShapeDtypeStruct((rows, own_width), jnp.bfloat16),
        ],
        in_specs=[VMEM] * (1 + len(a_held) + len(late)),
        out_specs=[VMEM, HBM],
        scratch_shapes=[
            pltpu.VMEM((rows, own_width), jnp.bfloat16),
            pltpu.SemaphoreType.DMA((rows // BS,)),
        ],
        input_output_aliases={0: 0},
        compiler_params=pltpu.CompilerParams(vmem_limit_bytes=8 << 20),
        name="late",
    )(total, *[v for v, _ in a_held], *[v for v, _ in late])
    return product


def solution(mesh):
    in_specs = (P("row", "col"), P("row", "col"), P("row", "col"), P("row", "col"))
    out_specs = P("row", ("col", "rep"))
    return jax.shard_map(
        functools.partial(per_device, dict(mesh.shape)),
        mesh=mesh,
        in_specs=in_specs,
        out_specs=out_specs,
        check_vma=False,
    )
```

time: 31.7 us -> 29.7 us (0.937)
  local copies, waits for them, and re-layouts: 2.13 us -> 0 us
  Pallas kernels: 3.26 us -> 4.33 us
  starting transfers between devices: 8.03 us -> 7.47 us
    unnamed x9 -> x0, local copies, waits for them, and re-layouts: 2.05 us -> none
    pallas_call x2 -> x3, Pallas kernels: 3.26 us -> 4.33 us  [the longest x1 1.72 us: per_device(): pl.pallas_call(functools.partial(prep_kernel, slots, block_rows, inner_lo...]
    ppermute x6, starting transfers between devices: 8.03 us -> 7.47 us  [the longest x3 4.42 us: per_device(): b_held.append((lax.ppermute(own_b, 'row', pairs), of))]
  transfers between devices with their start and end apart: 6 -> 6, of which waited for: 3 -> 4; matrix products, arithmetic and copies ran while one was open for 1% -> 0% of each run, Pallas kernels for 0% -> 3%
where the time goes in v2:
time: 29.7 us; the launch traced here: 29.6 us
  waiting for transfers between devices  17.8 us (60%)
  starting transfers between devices  7.47 us (25%)
  Pallas kernels  4.33 us (15%)
    ppermute x3, waiting for transfers between devices, per_device(): b_held.append((lax.ppermute(own_b, 'row', pairs), of))  11.3 us
    ppermute x3, waiting for transfers between devices, spread(): fresh.append((lax.ppermute(v, axis, pairs), mask ^ step))  6.47 us
    ppermute x3, starting transfers between devices, per_device(): b_held.append((lax.ppermute(own_b, 'row', pairs), of))  4.42 us
    ppermute x3, starting transfers between devices, spread(): fresh.append((lax.ppermute(v, axis, pairs), mask ^ step))  3.05 us
    pallas_call x1, Pallas kernels, per_device(): pl.pallas_call(functools.partial(prep_kernel, slots, block_rows, inner_lo...  1.72 us
    pallas_call x1, Pallas kernels, per_device(): pl.pallas_call(functools.partial(late_kernel, slots, inner_local, a_of, [...  1.62 us
    pallas_call x1, Pallas kernels, per_device(): pl.pallas_call(functools.partial(early_kernel, slots, inner_local, a_of,...  0.99 us
  transfers between devices with their start and end apart: 6, of which 4 were waited for; matrix products, arithmetic and copies ran while one was open for 0% of the time, Pallas kernels for 3%

profile of v2, /device:TPU:0, one launch (start us, length us, event | category | flops | bytes accessed | tf_op | source)
XLA Modules:
  0.0 29.6 jit_solution(5406743539689838849)
XLA Ops:
  0.0 1.7 %prep.1 = (bf16[528,256]{1,0:T(8,128)(2,1)S(1)}, bf16[256,256]{1,0:T(8,128)(2,1)S(1)}) custom-call(s32[1,8]{1,0:T(1,128)} %bitcast.1, bf16[2048,256]{1,0:T(8,128)(2,1)} %a_ref.1, s32[1,2]{1,0:T(1,128)} %bm_ref.1, bf16[256,512]{1,0:T(8,128)(2,1)} %b_ref.1), custom_call_target="tpu_custom_call" | custom-call | tf_op jit(solution)/shard_map/prep/pallas_call | solution.py:165
  1.7 3.0 %collective-permute-start = (bf16[528,256]{1,0:T(8,128)(2,1)S(1)}, bf16[528,256]{1,0:T(8,128)(2,1)S(1)}, u32[]{:S(2)}, u32[]{:S(2)}) collective-permute-start(bf16[528,256]{1,0:T(8,128)(2,1)S(1)} %get-tuple-element.8.refs_0_), channel_id=1, source_target_pairs={{0,4},{2,6},{4,0},{6,2},{1,5},{3,7},{5,1},{7,3},{8,12},{10,14},{12... | collective-permute-start | bytes 811016 | tf_op jit(solution)/shard_map/ppermute | solution.py:147
  4.8 0.0 collective-permute-start.1
  4.8 6.5 %collective-permute-done.refs_1_ = bf16[528,256]{1,0:T(8,128)(2,1)S(1)} collective-permute-done((bf16[528,256]{1,0:T(8,128)(2,1)S(1)}, bf16[528,256]{1,0:T(8,128)(2,1)S(1)}, u32[]{:S(2)}, u32[]{:S(2)}) %collective-permute-start) | collective-permute-done | bytes 270368 | tf_op jit(solution)/shard_map/ppermute | solution.py:147
  11.2 0.0 collective-permute-start.2
  11.2 1.8 %collective-permute-start.3 = (bf16[256,256]{1,0:T(8,128)(2,1)S(1)}, bf16[256,256]{1,0:T(8,128)(2,1)S(1)}, u32[]{:S(2)}, u32[]{:S(2)}) collective-permute-start(bf16[256,256]{1,0:T(8,128)(2,1)S(1)} %get-tuple-element.9.refs_4_), channel_id=1, source_target_pairs={{0,8},{8,0},{16,24},{24,16},{1,9},{9,1},{17,25},{25,17},{2,10},{10... | collective-permute-start | bytes 393224 | tf_op jit(solution)/shard_map/ppermute | solution.py:185
  13.1 2.5 %collective-permute-start.5 = (bf16[256,256]{1,0:T(8,128)(2,1)S(1)}, bf16[256,256]{1,0:T(8,128)(2,1)S(1)}, u32[]{:S(2)}, u32[]{:S(2)}) collective-permute-start(bf16[256,256]{1,0:T(8,128)(2,1)S(1)} %get-tuple-element.9.refs_4_), channel_id=1, source_target_pairs={{0,24},{8,16},{16,8},{24,0},{1,25},{9,17},{17,9},{25,1},{2,26},{10... | collective-permute-start | bytes 393224 | tf_op jit(solution)/shard_map/ppermute | solution.py:185
  15.5 0.1 collective-permute-start.4
  15.7 1.6 %collective-permute-done.3.refs_5_ = bf16[256,256]{1,0:T(8,128)(2,1)S(1)} collective-permute-done((bf16[256,256]{1,0:T(8,128)(2,1)S(1)}, bf16[256,256]{1,0:T(8,128)(2,1)S(1)}, u32[]{:S(2)}, u32[]{:S(2)}) %collective-permute-start.3) | collective-permute-done | bytes 131104 | tf_op jit(solution)/shard_map/ppermute | solution.py:185
  17.2 0.0 collective-permute-done.1.refs_2_
  17.2 0.0 collective-permute-done.2.refs_3_
  17.2 1.0 %early.1.total_ref = f32[2048,256]{1,0:T(8,128)S(1)} custom-call(bf16[528,256]{1,0:T(8,128)(2,1)S(1)} %get-tuple-element.8.refs_0_, bf16[528,256]{1,0:T(8,128)(2,1)S(1)} %collective-permute-done.refs_1_, bf16[528,256]{1,0:T(8,128)(2,1)S(1)} %collective-permute-done.1.refs_2_, bf16[528,256]{1,0:T(8,128)(2,1)S(1)} %collective-permute-done.2.refs_3_, ...), custom_call_target="tpu_custom_call" | custom-call | flops 1073741824 | bytes 4194304 | tf_op jit(solution)/shard_map/early/pallas_call | solution.py:190
  18.2 4.6 %collective-permute-done.5.refs_5_ = bf16[256,256]{1,0:T(8,128)(2,1)S(1)} collective-permute-done((bf16[256,256]{1,0:T(8,128)(2,1)S(1)}, bf16[256,256]{1,0:T(8,128)(2,1)S(1)}, u32[]{:S(2)}, u32[]{:S(2)}) %collective-permute-start.5) | collective-permute-done | bytes 131104 | tf_op jit(solution)/shard_map/ppermute | solution.py:185
  22.8 5.2 %collective-permute-done.4.refs_4_ = bf16[256,256]{1,0:T(8,128)(2,1)S(1)} collective-permute-done((bf16[256,256]{1,0:T(8,128)(2,1)S(1)}, bf16[256,256]{1,0:T(8,128)(2,1)S(1)}, u32[]{:S(2)}, u32[]{:S(2)}) %collective-permute-start.4) | collective-permute-done | bytes 131104 | tf_op jit(solution)/shard_map/ppermute | solution.py:185
  28.0 1.6 %late.1 = (f32[2048,256]{1,0:T(8,128)S(1)}, bf16[2048,256]{1,0:T(8,128)(2,1)}) custom-call(f32[2048,256]{1,0:T(8,128)S(1)} %early.1.total_ref, bf16[528,256]{1,0:T(8,128)(2,1)S(1)} %get-tuple-element.8.refs_0_, bf16[528,256]{1,0:T(8,128)(2,1)S(1)} %collective-permute-done.refs_1_, ...), custom_call_target="tpu_custom_call", output_to_operand_aliasing={{0}: (0, {})} | custom-call | tf_op jit(solution)/shard_map/late/pallas_call | solution.py:199
Async XLA Ops:
  1.7 9.5 %collective-permute-start = (bf16[528,256]{1,0:T(8,128)(2,1)S(1)}, bf16[528,256]{1,0:T(8,128)(2,1)S(1)}, u32[]{:S(2)}, u32[]{:S(2)}) collective-permute-start(bf16[528,256]{1,0:T(8,128)(2,1)S(1)} %get-tuple-element.8.refs_0_), channel_id=1, source_target_pairs={{0,4},{2,6},{4,0},{6,2},{1,5},{3,7},{5,1},{7,3},{8,12},{10,14},{12... | collective-permute-start | bytes 811016 | tf_op jit(solution)/shard_map/ppermute | solution.py:147
  4.8 12.5 %collective-permute-start.1 = (bf16[528,256]{1,0:T(8,128)(2,1)S(1)}, bf16[528,256]{1,0:T(8,128)(2,1)S(1)}, u32[]{:S(2)}, u32[]{:S(2)}) collective-permute-start(bf16[528,256]{1,0:T(8,128)(2,1)S(1)} %get-tuple-element.8.refs_0_), channel_id=1, source_target_pairs={{0,2},{2,0},{4,6},{6,4},{1,3},{3,1},{5,7},{7,5},{8,10},{10,8},{12,... | collective-permute-start | bytes 811016 | tf_op jit(solution)/shard_map/ppermute | solution.py:147
  11.2 6.0 %collective-permute-start.2 = (bf16[528,256]{1,0:T(8,128)(2,1)S(1)}, bf16[528,256]{1,0:T(8,128)(2,1)S(1)}, u32[]{:S(2)}, u32[]{:S(2)}) collective-permute-start(bf16[528,256]{1,0:T(8,128)(2,1)S(1)} %collective-permute-done.refs_1_), channel_id=1, source_target_pairs={{0,2},{2,0},{4,6},{6,4},{1,3},{3,1},{5,7},{7,5},{8,10},{10,8},{12,... | collective-permute-start | bytes 811016 | tf_op jit(solution)/shard_map/ppermute | solution.py:147
  11.2 6.0 %collective-permute-start.3 = (bf16[256,256]{1,0:T(8,128)(2,1)S(1)}, bf16[256,256]{1,0:T(8,128)(2,1)S(1)}, u32[]{:S(2)}, u32[]{:S(2)}) collective-permute-start(bf16[256,256]{1,0:T(8,128)(2,1)S(1)} %get-tuple-element.9.refs_4_), channel_id=1, source_target_pairs={{0,8},{8,0},{16,24},{24,16},{1,9},{9,1},{17,25},{25,17},{2,10},{10... | collective-permute-start | bytes 393224 | tf_op jit(solution)/shard_map/ppermute | solution.py:185
  13.1 9.7 %collective-permute-start.5 = (bf16[256,256]{1,0:T(8,128)(2,1)S(1)}, bf16[256,256]{1,0:T(8,128)(2,1)S(1)}, u32[]{:S(2)}, u32[]{:S(2)}) collective-permute-start(bf16[256,256]{1,0:T(8,128)(2,1)S(1)} %get-tuple-element.9.refs_4_), channel_id=1, source_target_pairs={{0,24},{8,16},{16,8},{24,0},{1,25},{9,17},{17,9},{25,1},{2,26},{10... | collective-permute-start | bytes 393224 | tf_op jit(solution)/shard_map/ppermute | solution.py:185
  15.5 12.4 %collective-permute-start.4 = (bf16[256,256]{1,0:T(8,128)(2,1)S(1)}, bf16[256,256]{1,0:T(8,128)(2,1)S(1)}, u32[]{:S(2)}, u32[]{:S(2)}) collective-permute-start(bf16[256,256]{1,0:T(8,128)(2,1)S(1)} %get-tuple-element.9.refs_4_), channel_id=1, source_target_pairs={{0,16},{8,24},{16,0},{24,8},{1,17},{9,25},{17,1},{25,9},{2,18},{10... | collective-permute-start | bytes 393224 | tf_op jit(solution)/shard_map/ppermute | solution.py:185

commit v3 on v2

--- a/solution.py
+++ b/solution.py
@@ -10,6 +10,7 @@
 
 BS = 256
 CODE_ALIGN = 16
+LATE = (1, 2)
 
 
 def block(index):
@@ -70,25 +71,32 @@
 def add_products(slots, inner_local, rows, a_refs, a_owners, b_refs, b_owners, total):
     cells = rows // BS * inner_local
     depth = b_refs[0].shape[0] // BS
-    found = []
+    groups = []
     for a_ref, owner in zip(a_refs, a_owners):
         codes = a_ref[pl.ds(slots * BS, CODE_ALIGN), pl.ds(0, 128)].astype(jnp.float32)
         index = lax.broadcasted_iota(jnp.int32, codes.shape, 0)
-        for slot in range(slots):
-            code = jnp.max(jnp.where(index == slot, codes, 0.0)).astype(jnp.int32)
-            row = code // inner_local if inner_local > 1 else code
-            inner = owner * inner_local + (code % inner_local if inner_local > 1 else 0)
-            found.append((a_ref, slot, code < cells, row, inner))
-    for a_ref, slot, used, row, inner in found:
+        places = [
+            jnp.max(jnp.where(index == slot, codes, 0.0)).astype(jnp.int32) for slot in range(slots)
+        ]
+        if inner_local == 1:
+            groups.append((a_ref, 0, places, owner))
+        else:
+            for slot, place in enumerate(places):
+                inside = jnp.where(place < cells, lax.rem(place, inner_local), 0)
+                groups.append((a_ref, slot, [place // inner_local], owner * inner_local + inside))
+    for a_ref, slot, places, inner in groups:
         for b_ref, owner in zip(b_refs, b_owners):
 
-            @pl.when(used & (inner // depth == owner))
+            @pl.when((inner // depth if depth > 1 else inner) == owner)
             def _():
-                inside = block(inner % depth) if depth > 1 else slice(None)
-                where = block(row)
-                total[where, :] += jnp.dot(
-                    a_ref[block(slot), :], b_ref[inside, :], preferred_element_type=jnp.float32
+                inside = block(lax.rem(inner, depth)) if depth > 1 else slice(None)
+                products = jnp.dot(
+                    a_ref[pl.ds(slot * BS, len(places) * BS), :],
+                    b_ref[inside, :],
+                    preferred_element_type=jnp.float32,
                 )
+                for at, row in enumerate(places):
+                    total[block(row), :] += products[at * BS : (at + 1) * BS]
 
 
 def early_kernel(slots, inner_local, a_of, b_of, *refs):
@@ -96,7 +104,7 @@
     total[...] = jnp.zeros_like(total)
     a_owners = [of(lax.axis_index("col")) for of in a_of]
     b_owners = [of(lax.axis_index("row")) for of in b_of]
-    add_products(slots, inner_local, total.shape[0], a_refs, a_owners, b_refs, b_owners, total)
+    add_products(slots, inner_local, total.shape[0] - BS, a_refs, a_owners, b_refs, b_owners, total)
 
 
 def late_kernel(slots, inner_local, a_of, b_of, total_ref, *refs):
@@ -104,9 +112,9 @@
     total, out_ref, stage, sem = refs[-4:]
     a_owners = [of(lax.axis_index("col")) for of in a_of]
     b_owners = [of(lax.axis_index("row")) for of in b_of]
-    add_products(slots, inner_local, total.shape[0], a_refs, a_owners, b_refs, b_owners, total)
+    add_products(slots, inner_local, total.shape[0] - BS, a_refs, a_owners, b_refs, b_owners, total)
     copies = []
-    for row in range(total.shape[0] // BS):
+    for row in range(out_ref.shape[0] // BS):
         stage[block(row), :] = total[block(row), :].astype(jnp.bfloat16)
         copies.append(
             pltpu.make_async_copy(stage.at[block(row), :], out_ref.at[block(row), :], sem.at[row])
@@ -124,11 +132,28 @@
     return lambda me: lax.rem(me + n - step, n)
 
 
-def hops(n):
+def route(n):
+    own = list(range(n))
     if n & (n - 1):
-        return [([(i, (i + s) % n) for i in range(n)], behind(s, n)) for s in range(1, n)]
-    order = list(range(n // 2, n)) + list(range(1, n // 2))
-    return [([(i, i ^ s) for i in range(n)], flip(s)) for s in order]
+        steps = [([(i, (i + s) % n) for i in own], None, s > n // 2) for s in range(1, n)]
+    else:
+        order = list(range(n // 2, n)) + list(range(1, n // 2))
+        steps = [([(i, i ^ s) for i in own], None, at in LATE) for at, s in enumerate(order)]
+    plan = []
+    for pairs, source, late in steps:
+        holds = {i: i for i in own} if source is None else plan[source][2]
+        plan.append((pairs, source, {dst: holds[src] for src, dst in pairs}, late))
+    return plan
+
+
+def owner_of(table):
+    def of(me):
+        owner = jnp.int32(-1)
+        for device, held in table.items():
+            owner = jnp.where(me == device, held, owner)
+        return owner
+
+    return of
 
 
 def spread(values, axis, n):
@@ -136,7 +161,8 @@
     held = [(values, same)]
     if n & (n - 1):
         return held + [
-            (lax.ppermute(values, axis, pairs), of) for pairs, of in hops(n)
+            (lax.ppermute(values, axis, [(i, (i + s) % n) for i in range(n)]), behind(s, n))
+            for s in range(1, n)
         ]
     step = n // 2
     masks = [(values, 0)]
@@ -180,16 +206,19 @@
         compiler_params=pltpu.CompilerParams(vmem_limit_bytes=60 << 20),
         name="prep",
     )(a_mask.T, a_blocks, b_mask, b_blocks)
-    b_held = [(own_b, lambda me: me)]
-    for pairs, of in hops(row_n):
-        b_held.append((lax.ppermute(own_b, "row", pairs), of))
+    plan = route(row_n)
+    arrived = []
+    for pairs, source, _, _ in plan:
+        sent = own_b if source is None else arrived[source]
+        arrived.append(lax.ppermute(sent, "row", pairs))
     a_held = spread(packed, "col", col_n)
-    far = -(-row_n // 2)
-    early, late = b_held[:1] + b_held[1 + far :], b_held[1 : 1 + far]
+    held = [(v, owner_of(step[2]), step[3]) for v, step in zip(arrived, plan)]
+    early = [(own_b, lambda me: me)] + [(v, of) for v, of, late in held if not late]
+    late = [(v, of) for v, of, late in held if late]
     a_of = [of for _, of in a_held]
     total = pl.pallas_call(
         functools.partial(early_kernel, slots, inner_local, a_of, [of for _, of in early]),
-        out_shape=jax.ShapeDtypeStruct((rows, own_width), jnp.float32),
+        out_shape=jax.ShapeDtypeStruct((rows + BS, own_width), jnp.float32),
         in_specs=[VMEM] * (len(a_held) + len(early)),
         out_specs=VMEM,
         compiler_params=pltpu.CompilerParams(vmem_limit_bytes=8 << 20),
@@ -199,7 +228,7 @@
     _, product = pl.pallas_call(
         functools.partial(late_kernel, slots, inner_local, a_of, [of for _, of in late]),
         out_shape=[
-            jax.ShapeDtypeStruct((rows, own_width), jnp.float32),
+            jax.ShapeDtypeStruct((rows + BS, own_width), jnp.float32),
             jax.ShapeDtypeStruct((rows, own_width), jnp.bfloat16),
         ],
         in_specs=[VMEM] * (1 + len(a_held) + len(late)),

time: 29.7 us -> 27.3 us (0.919)
  the two profiles are of different devices: /device:TPU:0 before, /device:TPU:21 now
where the time goes in v3:
time: 27.3 us; the launch traced here: 27.2 us
  waiting for transfers between devices  16.6 us (61%)
  starting transfers between devices  6.41 us (23%)
  Pallas kernels  4.14 us (15%)
    ppermute x3, waiting for transfers between devices, per_device(): arrived.append(lax.ppermute(sent, 'row', pairs))  11.4 us
    ppermute x3, waiting for transfers between devices, spread(): fresh.append((lax.ppermute(v, axis, pairs), mask ^ step))  5.2 us
    ppermute x3, starting transfers between devices, spread(): fresh.append((lax.ppermute(v, axis, pairs), mask ^ step))  3.76 us
    ppermute x3, starting transfers between devices, per_device(): arrived.append(lax.ppermute(sent, 'row', pairs))  2.65 us
    pallas_call x1, Pallas kernels, per_device(): pl.pallas_call(functools.partial(prep_kernel, slots, block_rows, inner_lo...  1.72 us
    pallas_call x1, Pallas kernels, per_device(): pl.pallas_call(functools.partial(late_kernel, slots, inner_local, a_of, [...  1.7 us
    pallas_call x1, Pallas kernels, per_device(): pl.pallas_call(functools.partial(early_kernel, slots, inner_local, a_of,...  0.72 us
  transfers between devices with their start and end apart: 6, of which 4 were waited for; matrix products, arithmetic and copies ran while one was open for 0% of the time, Pallas kernels for 3%

profile of v3, /device:TPU:21, one launch (start us, length us, event | category | flops | bytes accessed | tf_op | source)
XLA Modules:
  0.0 27.2 jit_solution(3056343539427836676)
XLA Ops:
  0.0 1.7 %prep.1 = (bf16[528,256]{1,0:T(8,128)(2,1)S(1)}, bf16[256,256]{1,0:T(8,128)(2,1)S(1)}) custom-call(s32[1,8]{1,0:T(1,128)} %bitcast.1, bf16[2048,256]{1,0:T(8,128)(2,1)} %a_ref.1, s32[1,2]{1,0:T(1,128)} %bm_ref.1, bf16[256,512]{1,0:T(8,128)(2,1)} %b_ref.1), custom_call_target="tpu_custom_call" | custom-call | tf_op jit(solution)/shard_map/prep/pallas_call | solution.py:191
  1.7 1.3 %collective-permute-start = (bf16[528,256]{1,0:T(8,128)(2,1)S(1)}, bf16[528,256]{1,0:T(8,128)(2,1)S(1)}, u32[]{:S(2)}, u32[]{:S(2)}) collective-permute-start(bf16[528,256]{1,0:T(8,128)(2,1)S(1)} %get-tuple-element.8.refs_0_), channel_id=1, source_target_pairs={{0,4},{2,6},{4,0},{6,2},{1,5},{3,7},{5,1},{7,3},{8,12},{10,14},{12... | collective-permute-start | bytes 811016 | tf_op jit(solution)/shard_map/ppermute | solution.py:173
  3.0 1.0 %collective-permute-start.1 = (bf16[528,256]{1,0:T(8,128)(2,1)S(1)}, bf16[528,256]{1,0:T(8,128)(2,1)S(1)}, u32[]{:S(2)}, u32[]{:S(2)}) collective-permute-start(bf16[528,256]{1,0:T(8,128)(2,1)S(1)} %get-tuple-element.8.refs_0_), channel_id=1, source_target_pairs={{0,2},{2,0},{4,6},{6,4},{1,3},{3,1},{5,7},{7,5},{8,10},{10,8},{12,... | collective-permute-start | bytes 811016 | tf_op jit(solution)/shard_map/ppermute | solution.py:173
  4.0 5.2 %collective-permute-done.refs_1_ = bf16[528,256]{1,0:T(8,128)(2,1)S(1)} collective-permute-done((bf16[528,256]{1,0:T(8,128)(2,1)S(1)}, bf16[528,256]{1,0:T(8,128)(2,1)S(1)}, u32[]{:S(2)}, u32[]{:S(2)}) %collective-permute-start) | collective-permute-done | bytes 270368 | tf_op jit(solution)/shard_map/ppermute | solution.py:173
  9.2 1.5 %collective-permute-start.2 = (bf16[528,256]{1,0:T(8,128)(2,1)S(1)}, bf16[528,256]{1,0:T(8,128)(2,1)S(1)}, u32[]{:S(2)}, u32[]{:S(2)}) collective-permute-start(bf16[528,256]{1,0:T(8,128)(2,1)S(1)} %collective-permute-done.refs_1_), channel_id=1, source_target_pairs={{0,2},{2,0},{4,6},{6,4},{1,3},{3,1},{5,7},{7,5},{8,10},{10,8},{12,... | collective-permute-start | bytes 811016 | tf_op jit(solution)/shard_map/ppermute | solution.py:173
  10.7 0.1 collective-permute-start.3
  10.7 1.3 %collective-permute-start.5 = (bf16[256,256]{1,0:T(8,128)(2,1)S(1)}, bf16[256,256]{1,0:T(8,128)(2,1)S(1)}, u32[]{:S(2)}, u32[]{:S(2)}) collective-permute-start(bf16[256,256]{1,0:T(8,128)(2,1)S(1)} %get-tuple-element.9.refs_4_), channel_id=1, source_target_pairs={{0,8},{8,0},{16,24},{24,16},{1,9},{9,1},{17,25},{25,17},{2,10},{10... | collective-permute-start | bytes 393224 | tf_op jit(solution)/shard_map/ppermute | solution.py:213
  12.0 1.3 %collective-permute-start.4 = (bf16[256,256]{1,0:T(8,128)(2,1)S(1)}, bf16[256,256]{1,0:T(8,128)(2,1)S(1)}, u32[]{:S(2)}, u32[]{:S(2)}) collective-permute-start(bf16[256,256]{1,0:T(8,128)(2,1)S(1)} %get-tuple-element.9.refs_4_), channel_id=1, source_target_pairs={{0,24},{8,16},{16,8},{24,0},{1,25},{9,17},{17,9},{25,1},{2,26},{10... | collective-permute-start | bytes 393224 | tf_op jit(solution)/shard_map/ppermute | solution.py:213
  13.3 3.3 %collective-permute-done.3.refs_5_ = bf16[256,256]{1,0:T(8,128)(2,1)S(1)} collective-permute-done((bf16[256,256]{1,0:T(8,128)(2,1)S(1)}, bf16[256,256]{1,0:T(8,128)(2,1)S(1)}, u32[]{:S(2)}, u32[]{:S(2)}) %collective-permute-start.3) | collective-permute-done | bytes 131104 | tf_op jit(solution)/shard_map/ppermute | solution.py:213
  16.7 0.0 collective-permute-done.1.refs_2_
  16.7 0.0 collective-permute-done.2.refs_3_
  16.7 0.7 %early.1.total_ref = f32[2304,256]{1,0:T(8,128)S(1)} custom-call(bf16[528,256]{1,0:T(8,128)(2,1)S(1)} %get-tuple-element.8.refs_0_, bf16[528,256]{1,0:T(8,128)(2,1)S(1)} %collective-permute-done.refs_1_, bf16[528,256]{1,0:T(8,128)(2,1)S(1)} %collective-permute-done.1.refs_2_, bf16[528,256]{1,0:T(8,128)(2,1)S(1)} %collective-permute-done.2.refs_3_, ...), custom_call_target="tpu_custom_call" | custom-call | flops 1073741824 | bytes 4194304 | tf_op jit(solution)/shard_map/early/pallas_call | solution.py:219
  17.4 1.1 %collective-permute-done.5.refs_5_ = bf16[256,256]{1,0:T(8,128)(2,1)S(1)} collective-permute-done((bf16[256,256]{1,0:T(8,128)(2,1)S(1)}, bf16[256,256]{1,0:T(8,128)(2,1)S(1)}, u32[]{:S(2)}, u32[]{:S(2)}) %collective-permute-start.5) | collective-permute-done | bytes 131104 | tf_op jit(solution)/shard_map/ppermute | solution.py:213
  18.5 7.0 %collective-permute-done.4.refs_4_ = bf16[256,256]{1,0:T(8,128)(2,1)S(1)} collective-permute-done((bf16[256,256]{1,0:T(8,128)(2,1)S(1)}, bf16[256,256]{1,0:T(8,128)(2,1)S(1)}, u32[]{:S(2)}, u32[]{:S(2)}) %collective-permute-start.4) | collective-permute-done | bytes 131104 | tf_op jit(solution)/shard_map/ppermute | solution.py:213
  25.5 1.7 %late.1 = (f32[2304,256]{1,0:T(8,128)S(1)}, bf16[2048,256]{1,0:T(8,128)(2,1)}) custom-call(f32[2304,256]{1,0:T(8,128)S(1)} %early.1.total_ref, bf16[528,256]{1,0:T(8,128)(2,1)S(1)} %get-tuple-element.8.refs_0_, bf16[528,256]{1,0:T(8,128)(2,1)S(1)} %collective-permute-done.refs_1_, ...), custom_call_target="tpu_custom_call", output_to_operand_aliasing={{0}: (0, {})} | custom-call | tf_op jit(solution)/shard_map/late/pallas_call | solution.py:228
Async XLA Ops:
  1.7 7.4 %collective-permute-start = (bf16[528,256]{1,0:T(8,128)(2,1)S(1)}, bf16[528,256]{1,0:T(8,128)(2,1)S(1)}, u32[]{:S(2)}, u32[]{:S(2)}) collective-permute-start(bf16[528,256]{1,0:T(8,128)(2,1)S(1)} %get-tuple-element.8.refs_0_), channel_id=1, source_target_pairs={{0,4},{2,6},{4,0},{6,2},{1,5},{3,7},{5,1},{7,3},{8,12},{10,14},{12... | collective-permute-start | bytes 811016 | tf_op jit(solution)/shard_map/ppermute | solution.py:173
  3.0 13.7 %collective-permute-start.1 = (bf16[528,256]{1,0:T(8,128)(2,1)S(1)}, bf16[528,256]{1,0:T(8,128)(2,1)S(1)}, u32[]{:S(2)}, u32[]{:S(2)}) collective-permute-start(bf16[528,256]{1,0:T(8,128)(2,1)S(1)} %get-tuple-element.8.refs_0_), channel_id=1, source_target_pairs={{0,2},{2,0},{4,6},{6,4},{1,3},{3,1},{5,7},{7,5},{8,10},{10,8},{12,... | collective-permute-start | bytes 811016 | tf_op jit(solution)/shard_map/ppermute | solution.py:173
  9.2 7.5 %collective-permute-start.2 = (bf16[528,256]{1,0:T(8,128)(2,1)S(1)}, bf16[528,256]{1,0:T(8,128)(2,1)S(1)}, u32[]{:S(2)}, u32[]{:S(2)}) collective-permute-start(bf16[528,256]{1,0:T(8,128)(2,1)S(1)} %collective-permute-done.refs_1_), channel_id=1, source_target_pairs={{0,2},{2,0},{4,6},{6,4},{1,3},{3,1},{5,7},{7,5},{8,10},{10,8},{12,... | collective-permute-start | bytes 811016 | tf_op jit(solution)/shard_map/ppermute | solution.py:173
  10.7 6.0 %collective-permute-start.3 = (bf16[256,256]{1,0:T(8,128)(2,1)S(1)}, bf16[256,256]{1,0:T(8,128)(2,1)S(1)}, u32[]{:S(2)}, u32[]{:S(2)}) collective-permute-start(bf16[256,256]{1,0:T(8,128)(2,1)S(1)} %get-tuple-element.9.refs_4_), channel_id=1, source_target_pairs={{0,16},{8,24},{16,0},{24,8},{1,17},{9,25},{17,1},{25,9},{2,18},{10... | collective-permute-start | bytes 393224 | tf_op jit(solution)/shard_map/ppermute | solution.py:213
  10.7 7.7 %collective-permute-start.5 = (bf16[256,256]{1,0:T(8,128)(2,1)S(1)}, bf16[256,256]{1,0:T(8,128)(2,1)S(1)}, u32[]{:S(2)}, u32[]{:S(2)}) collective-permute-start(bf16[256,256]{1,0:T(8,128)(2,1)S(1)} %get-tuple-element.9.refs_4_), channel_id=1, source_target_pairs={{0,8},{8,0},{16,24},{24,16},{1,9},{9,1},{17,25},{25,17},{2,10},{10... | collective-permute-start | bytes 393224 | tf_op jit(solution)/shard_map/ppermute | solution.py:213
  12.0 13.4 %collective-permute-start.4 = (bf16[256,256]{1,0:T(8,128)(2,1)S(1)}, bf16[256,256]{1,0:T(8,128)(2,1)S(1)}, u32[]{:S(2)}, u32[]{:S(2)}) collective-permute-start(bf16[256,256]{1,0:T(8,128)(2,1)S(1)} %get-tuple-element.9.refs_4_), channel_id=1, source_target_pairs={{0,24},{8,16},{16,8},{24,0},{1,25},{9,17},{17,9},{25,1},{2,26},{10... | collective-permute-start | bytes 393224 | tf_op jit(solution)/shard_map/ppermute | solution.py:213

commit v4 on v3

--- a/solution.py
+++ b/solution.py
@@ -18,7 +18,7 @@
     return pl.ds(start if isinstance(index, int) else pl.multiple_of(start, BS), BS)
 
 
-def prep_kernel(slots, rows, cols, am_ref, a_ref, bm_ref, b_ref, pack_ref, own_ref, am, bm, a_sem, b_sem, m_sem):
+def prep_kernel(slots, rows, cols, am_ref, a_ref, bm_ref, b_ref, pack_ref, own_ref, am, bm, tile, a_sem, b_sem, m_sem):
     width = own_ref.shape[1]
     wide = width // BS
     layer = lax.axis_index("rep")
@@ -30,6 +30,8 @@
     load_am.start()
     load_bm.start()
     load_b.start()
+    load_a = pltpu.make_async_copy(a_ref, tile, a_sem)
+    load_a.start()
     load_am.wait()
     cells = rows * cols
     place = [jnp.int32(cells)] * slots
@@ -39,18 +41,13 @@
         for slot in range(slots):
             place[slot] = jnp.where(hit & (count == slot), cell, place[slot])
         count = count + hit.astype(jnp.int32)
-    copies = []
+    load_a.wait()
     for slot in range(slots):
         cell = jnp.minimum(place[slot], cells - 1)
-        across = block(cell % cols) if cols > 1 else slice(None)
-        copies.append(
-            pltpu.make_async_copy(
-                a_ref.at[block(cell // cols if cols > 1 else cell), across],
-                pack_ref.at[block(slot), :],
-                a_sem.at[slot],
-            )
-        )
-        copies[-1].start()
+        if cols == 1:
+            pack_ref[block(slot), :] = tile[block(cell), :]
+        else:
+            pack_ref[block(slot), :] = tile[block(cell // cols), block(lax.rem(cell, cols))]
     code_rows = pack_ref.shape[0] - slots * BS
     index = lax.broadcasted_iota(jnp.int32, (code_rows, BS), 0)
     codes = jnp.full((code_rows, BS), cells, jnp.int32)
@@ -64,20 +61,23 @@
             keep = bm[down, layer * wide + over].astype(jnp.float32)
             part = (block(down), block(over))
             own_ref[part] = (own_ref[part].astype(jnp.float32) * keep).astype(jnp.bfloat16)
-    for copy in copies:
-        copy.wait()
-
-
-def add_products(slots, inner_local, rows, a_refs, a_owners, b_refs, b_owners, total):
-    cells = rows // BS * inner_local
+
+
+def read_places(slots, a_refs, places_ref):
+    for at, a_ref in enumerate(a_refs):
+        codes = a_ref[pl.ds(slots * BS, CODE_ALIGN), pl.ds(0, 128)].astype(jnp.float32)
+        index = lax.broadcasted_iota(jnp.int32, codes.shape, 0)
+        for slot in range(slots):
+            place = jnp.max(jnp.where(index == slot, codes, 0.0)).astype(jnp.int32)
+            places_ref[at * slots + slot] = place
+
+
+def add_products(slots, inner_local, places_ref, a_refs, a_owners, b_refs, b_owners, total):
+    cells = (total.shape[0] // BS - 1) * inner_local
     depth = b_refs[0].shape[0] // BS
     groups = []
-    for a_ref, owner in zip(a_refs, a_owners):
-        codes = a_ref[pl.ds(slots * BS, CODE_ALIGN), pl.ds(0, 128)].astype(jnp.float32)
-        index = lax.broadcasted_iota(jnp.int32, codes.shape, 0)
-        places = [
-            jnp.max(jnp.where(index == slot, codes, 0.0)).astype(jnp.int32) for slot in range(slots)
-        ]
+    for at, (a_ref, owner) in enumerate(zip(a_refs, a_owners)):
+        places = [places_ref[at * slots + slot] for slot in range(slots)]
         if inner_local == 1:
             groups.append((a_ref, 0, places, owner))
         else:
@@ -100,19 +100,21 @@
 
 
 def early_kernel(slots, inner_local, a_of, b_of, *refs):
-    a_refs, b_refs, total = refs[: len(a_of)], refs[len(a_of) : -1], refs[-1]
+    a_refs, b_refs = refs[: len(a_of)], refs[len(a_of) : -2]
+    total, places_ref = refs[-2:]
     total[...] = jnp.zeros_like(total)
+    read_places(slots, a_refs, places_ref)
     a_owners = [of(lax.axis_index("col")) for of in a_of]
     b_owners = [of(lax.axis_index("row")) for of in b_of]
-    add_products(slots, inner_local, total.shape[0] - BS, a_refs, a_owners, b_refs, b_owners, total)
-
-
-def late_kernel(slots, inner_local, a_of, b_of, total_ref, *refs):
+    add_products(slots, inner_local, places_ref, a_refs, a_owners, b_refs, b_owners, total)
+
+
+def late_kernel(slots, inner_local, a_of, b_of, total_ref, places_ref, *refs):
     a_refs, b_refs = refs[: len(a_of)], refs[len(a_of) : -4]
     total, out_ref, stage, sem = refs[-4:]
     a_owners = [of(lax.axis_index("col")) for of in a_of]
     b_owners = [of(lax.axis_index("row")) for of in b_of]
-    add_products(slots, inner_local, total.shape[0] - BS, a_refs, a_owners, b_refs, b_owners, total)
+    add_products(slots, inner_local, places_ref, a_refs, a_owners, b_refs, b_owners, total)
     copies = []
     for row in range(out_ref.shape[0] // BS):
         stage[block(row), :] = total[block(row), :].astype(jnp.bfloat16)
@@ -177,6 +179,7 @@
 
 
 VMEM = pl.BlockSpec(memory_space=pltpu.VMEM)
+SMEM = pl.BlockSpec(memory_space=pltpu.SMEM)
 HBM = pl.BlockSpec(memory_space=pltpu.HBM)
 
 
@@ -199,7 +202,8 @@
         scratch_shapes=[
             pltpu.SMEM(a_mask.shape[::-1], jnp.int32),
             pltpu.SMEM(b_mask.shape, jnp.int32),
-            pltpu.SemaphoreType.DMA((slots,)),
+            pltpu.VMEM(a_blocks.shape, jnp.bfloat16),
+            pltpu.SemaphoreType.DMA,
             pltpu.SemaphoreType.DMA,
             pltpu.SemaphoreType.DMA((2,)),
         ],
@@ -216,11 +220,14 @@
     early = [(own_b, lambda me: me)] + [(v, of) for v, of, late in held if not late]
     late = [(v, of) for v, of, late in held if late]
     a_of = [of for _, of in a_held]
-    total = pl.pallas_call(
+    total, places = pl.pallas_call(
         functools.partial(early_kernel, slots, inner_local, a_of, [of for _, of in early]),
-        out_shape=jax.ShapeDtypeStruct((rows + BS, own_width), jnp.float32),
+        out_shape=[
+            jax.ShapeDtypeStruct((rows + BS, own_width), jnp.float32),
+            pltpu.SMEM((len(a_held) * slots,), jnp.int32),
+        ],
         in_specs=[VMEM] * (len(a_held) + len(early)),
-        out_specs=VMEM,
+        out_specs=[VMEM, SMEM],
         compiler_params=pltpu.CompilerParams(vmem_limit_bytes=8 << 20),
         cost_estimate=pl.CostEstimate(flops=1 << 30, bytes_accessed=1 << 22, transcendentals=0),
         name="early",
@@ -231,7 +238,7 @@
             jax.ShapeDtypeStruct((rows + BS, own_width), jnp.float32),
             jax.ShapeDtypeStruct((rows, own_width), jnp.bfloat16),
         ],
-        in_specs=[VMEM] * (1 + len(a_held) + len(late)),
+        in_specs=[VMEM, SMEM] + [VMEM] * (len(a_held) + len(late)),
         out_specs=[VMEM, HBM],
         scratch_shapes=[
             pltpu.VMEM((rows, own_width), jnp.bfloat16),
@@ -240,7 +247,7 @@
         input_output_aliases={0: 0},
         compiler_params=pltpu.CompilerParams(vmem_limit_bytes=8 << 20),
         name="late",
-    )(total, *[v for v, _ in a_held], *[v for v, _ in late])
+    )(total, places, *[v for v, _ in a_held], *[v for v, _ in late])
     return product
 
 

time: 27.3 us -> 26.8 us (0.982)
  the two profiles are of different devices: /device:TPU:21 before, /device:TPU:19 now
where the time goes in v4:
time: 26.8 us; the launch traced here: 26.7 us
  waiting for transfers between devices  17.6 us (66%)
  starting transfers between devices  5.45 us (20%)
  Pallas kernels  3.62 us (14%)
    ppermute x3, waiting for transfers between devices, per_device(): arrived.append(lax.ppermute(sent, 'row', pairs))  11.4 us
    ppermute x3, waiting for transfers between devices, spread(): fresh.append((lax.ppermute(v, axis, pairs), mask ^ step))  6.16 us
    ppermute x3, starting transfers between devices, spread(): fresh.append((lax.ppermute(v, axis, pairs), mask ^ step))  2.81 us
    ppermute x3, starting transfers between devices, per_device(): arrived.append(lax.ppermute(sent, 'row', pairs))  2.65 us
    pallas_call x1, Pallas kernels, per_device(): pl.pallas_call(functools.partial(late_kernel, slots, inner_local, a_of, [...  1.57 us
    pallas_call x1, Pallas kernels, per_device(): pl.pallas_call(functools.partial(prep_kernel, slots, block_rows, inner_lo...  1.31 us
    pallas_call x1, Pallas kernels, per_device(): pl.pallas_call(functools.partial(early_kernel, slots, inner_local, a_of,...  0.74 us
  transfers between devices with their start and end apart: 6, of which 4 were waited for; matrix products, arithmetic and copies ran while one was open for 0% of the time, Pallas kernels for 3%

profile of v4, /device:TPU:19, one launch (start us, length us, event | category | flops | bytes accessed | tf_op | source)
XLA Modules:
  0.0 26.7 jit_solution(16731669482710193192)
XLA Ops:
  0.0 1.3 %prep.1 = (bf16[528,256]{1,0:T(8,128)(2,1)S(1)}, bf16[256,256]{1,0:T(8,128)(2,1)S(1)}) custom-call(s32[1,8]{1,0:T(1,128)} %bitcast.1, bf16[2048,256]{1,0:T(8,128)(2,1)} %a_ref.1, s32[1,2]{1,0:T(1,128)} %bm_ref.1, bf16[256,512]{1,0:T(8,128)(2,1)} %b_ref.1), custom_call_target="tpu_custom_call" | custom-call | tf_op jit(solution)/shard_map/prep/pallas_call | solution.py:194
  1.3 0.3 %collective-permute-start = (bf16[528,256]{1,0:T(8,128)(2,1)S(1)}, bf16[528,256]{1,0:T(8,128)(2,1)S(1)}, u32[]{:S(2)}, u32[]{:S(2)}) collective-permute-start(bf16[528,256]{1,0:T(8,128)(2,1)S(1)} %get-tuple-element.10.refs_0_), channel_id=1, source_target_pairs={{0,4},{2,6},{4,0},{6,2},{1,5},{3,7},{5,1},{7,3},{8,12},{10,14},{12... | collective-permute-start | bytes 811016 | tf_op jit(solution)/shard_map/ppermute | solution.py:175
  1.6 1.0 %collective-permute-start.1 = (bf16[528,256]{1,0:T(8,128)(2,1)S(1)}, bf16[528,256]{1,0:T(8,128)(2,1)S(1)}, u32[]{:S(2)}, u32[]{:S(2)}) collective-permute-start(bf16[528,256]{1,0:T(8,128)(2,1)S(1)} %get-tuple-element.10.refs_0_), channel_id=1, source_target_pairs={{0,2},{2,0},{4,6},{6,4},{1,3},{3,1},{5,7},{7,5},{8,10},{10,8},{12,... | collective-permute-start | bytes 811016 | tf_op jit(solution)/shard_map/ppermute | solution.py:175
  2.6 6.2 %collective-permute-done.refs_1_ = bf16[528,256]{1,0:T(8,128)(2,1)S(1)} collective-permute-done((bf16[528,256]{1,0:T(8,128)(2,1)S(1)}, bf16[528,256]{1,0:T(8,128)(2,1)S(1)}, u32[]{:S(2)}, u32[]{:S(2)}) %collective-permute-start) | collective-permute-done | bytes 270368 | tf_op jit(solution)/shard_map/ppermute | solution.py:175
  8.8 1.5 %collective-permute-start.2 = (bf16[528,256]{1,0:T(8,128)(2,1)S(1)}, bf16[528,256]{1,0:T(8,128)(2,1)S(1)}, u32[]{:S(2)}, u32[]{:S(2)}) collective-permute-start(bf16[528,256]{1,0:T(8,128)(2,1)S(1)} %collective-permute-done.refs_1_), channel_id=1, source_target_pairs={{0,2},{2,0},{4,6},{6,4},{1,3},{3,1},{5,7},{7,5},{8,10},{10,8},{12,... | collective-permute-start | bytes 811016 | tf_op jit(solution)/shard_map/ppermute | solution.py:175
  10.3 0.1 collective-permute-start.3
  10.3 1.3 %collective-permute-start.5 = (bf16[256,256]{1,0:T(8,128)(2,1)S(1)}, bf16[256,256]{1,0:T(8,128)(2,1)S(1)}, u32[]{:S(2)}, u32[]{:S(2)}) collective-permute-start(bf16[256,256]{1,0:T(8,128)(2,1)S(1)} %get-tuple-element.11.refs_4_), channel_id=1, source_target_pairs={{0,8},{8,0},{16,24},{24,16},{1,9},{9,1},{17,25},{25,17},{2,10},{10... | collective-permute-start | bytes 393224 | tf_op jit(solution)/shard_map/ppermute | solution.py:217
  11.6 1.3 %collective-permute-start.4 = (bf16[256,256]{1,0:T(8,128)(2,1)S(1)}, bf16[256,256]{1,0:T(8,128)(2,1)S(1)}, u32[]{:S(2)}, u32[]{:S(2)}) collective-permute-start(bf16[256,256]{1,0:T(8,128)(2,1)S(1)} %get-tuple-element.11.refs_4_), channel_id=1, source_target_pairs={{0,24},{8,16},{16,8},{24,0},{1,25},{9,17},{17,9},{25,1},{2,26},{10... | collective-permute-start | bytes 393224 | tf_op jit(solution)/shard_map/ppermute | solution.py:217
  12.9 3.3 %collective-permute-done.3.refs_5_ = bf16[256,256]{1,0:T(8,128)(2,1)S(1)} collective-permute-done((bf16[256,256]{1,0:T(8,128)(2,1)S(1)}, bf16[256,256]{1,0:T(8,128)(2,1)S(1)}, u32[]{:S(2)}, u32[]{:S(2)}) %collective-permute-start.3) | collective-permute-done | bytes 131104 | tf_op jit(solution)/shard_map/ppermute | solution.py:217
  16.3 0.0 collective-permute-done.1.refs_2_
  16.3 0.0 collective-permute-done.2.refs_3_
  16.3 0.7 %early.1 = (f32[2304,256]{1,0:T(8,128)S(1)}, s32[8]{0:T(128)S(4)}) custom-call(bf16[528,256]{1,0:T(8,128)(2,1)S(1)} %get-tuple-element.10.refs_0_, bf16[528,256]{1,0:T(8,128)(2,1)S(1)} %collective-permute-done.refs_1_, bf16[528,256]{1,0:T(8,128)(2,1)S(1)} %collective-permute-done.1.refs_2_, bf16[528,256]{1,0:T(8,128)(2,1)S(1)} %collective-permute-done.2.refs_3_, ...), custom_call_target="tpu_custom_call" | custom-call | flops 1073741824 | bytes 4194304 | tf_op jit(solution)/shard_map/early/pallas_call | solution.py:223
  17.0 1.0 %collective-permute-done.5.refs_5_ = bf16[256,256]{1,0:T(8,128)(2,1)S(1)} collective-permute-done((bf16[256,256]{1,0:T(8,128)(2,1)S(1)}, bf16[256,256]{1,0:T(8,128)(2,1)S(1)}, u32[]{:S(2)}, u32[]{:S(2)}) %collective-permute-start.5) | collective-permute-done | bytes 131104 | tf_op jit(solution)/shard_map/ppermute | solution.py:217
  18.1 7.0 %collective-permute-done.4.refs_4_ = bf16[256,256]{1,0:T(8,128)(2,1)S(1)} collective-permute-done((bf16[256,256]{1,0:T(8,128)(2,1)S(1)}, bf16[256,256]{1,0:T(8,128)(2,1)S(1)}, u32[]{:S(2)}, u32[]{:S(2)}) %collective-permute-start.4) | collective-permute-done | bytes 131104 | tf_op jit(solution)/shard_map/ppermute | solution.py:217
  25.1 1.6 %late.1 = (f32[2304,256]{1,0:T(8,128)S(1)}, bf16[2048,256]{1,0:T(8,128)(2,1)}) custom-call(f32[2304,256]{1,0:T(8,128)S(1)} %get-tuple-element.12.total_ref, s32[8]{0:T(128)S(4)} %get-tuple-element.13.places_ref, bf16[528,256]{1,0:T(8,128)(2,1)S(1)} %get-tuple-element.10.refs_0_, ...), custom_call_target="tpu_custom_call", output_to_operand_aliasing={{0}: (0, {})} | custom-call | tf_op jit(solution)/shard_map/late/pallas_call | solution.py:235
Async XLA Ops:
  1.3 7.4 %collective-permute-start = (bf16[528,256]{1,0:T(8,128)(2,1)S(1)}, bf16[528,256]{1,0:T(8,128)(2,1)S(1)}, u32[]{:S(2)}, u32[]{:S(2)}) collective-permute-start(bf16[528,256]{1,0:T(8,128)(2,1)S(1)} %get-tuple-element.10.refs_0_), channel_id=1, source_target_pairs={{0,4},{2,6},{4,0},{6,2},{1,5},{3,7},{5,1},{7,3},{8,12},{10,14},{12... | collective-permute-start | bytes 811016 | tf_op jit(solution)/shard_map/ppermute | solution.py:175
  1.6 14.6 %collective-permute-start.1 = (bf16[528,256]{1,0:T(8,128)(2,1)S(1)}, bf16[528,256]{1,0:T(8,128)(2,1)S(1)}, u32[]{:S(2)}, u32[]{:S(2)}) collective-permute-start(bf16[528,256]{1,0:T(8,128)(2,1)S(1)} %get-tuple-element.10.refs_0_), channel_id=1, source_target_pairs={{0,2},{2,0},{4,6},{6,4},{1,3},{3,1},{5,7},{7,5},{8,10},{10,8},{12,... | collective-permute-start | bytes 811016 | tf_op jit(solution)/shard_map/ppermute | solution.py:175
  8.8 7.5 %collective-permute-start.2 = (bf16[528,256]{1,0:T(8,128)(2,1)S(1)}, bf16[528,256]{1,0:T(8,128)(2,1)S(1)}, u32[]{:S(2)}, u32[]{:S(2)}) collective-permute-start(bf16[528,256]{1,0:T(8,128)(2,1)S(1)} %collective-permute-done.refs_1_), channel_id=1, source_target_pairs={{0,2},{2,0},{4,6},{6,4},{1,3},{3,1},{5,7},{7,5},{8,10},{10,8},{12,... | collective-permute-start | bytes 811016 | tf_op jit(solution)/shard_map/ppermute | solution.py:175
  10.3 6.0 %collective-permute-start.3 = (bf16[256,256]{1,0:T(8,128)(2,1)S(1)}, bf16[256,256]{1,0:T(8,128)(2,1)S(1)}, u32[]{:S(2)}, u32[]{:S(2)}) collective-permute-start(bf16[256,256]{1,0:T(8,128)(2,1)S(1)} %get-tuple-element.11.refs_4_), channel_id=1, source_target_pairs={{0,16},{8,24},{16,0},{24,8},{1,17},{9,25},{17,1},{25,9},{2,18},{10... | collective-permute-start | bytes 393224 | tf_op jit(solution)/shard_map/ppermute | solution.py:217
  10.3 7.7 %collective-permute-start.5 = (bf16[256,256]{1,0:T(8,128)(2,1)S(1)}, bf16[256,256]{1,0:T(8,128)(2,1)S(1)}, u32[]{:S(2)}, u32[]{:S(2)}) collective-permute-start(bf16[256,256]{1,0:T(8,128)(2,1)S(1)} %get-tuple-element.11.refs_4_), channel_id=1, source_target_pairs={{0,8},{8,0},{16,24},{24,16},{1,9},{9,1},{17,25},{25,17},{2,10},{10... | collective-permute-start | bytes 393224 | tf_op jit(solution)/shard_map/ppermute | solution.py:217
  11.6 13.4 %collective-permute-start.4 = (bf16[256,256]{1,0:T(8,128)(2,1)S(1)}, bf16[256,256]{1,0:T(8,128)(2,1)S(1)}, u32[]{:S(2)}, u32[]{:S(2)}) collective-permute-start(bf16[256,256]{1,0:T(8,128)(2,1)S(1)} %get-tuple-element.11.refs_4_), channel_id=1, source_target_pairs={{0,24},{8,16},{16,8},{24,0},{1,25},{9,17},{17,9},{25,1},{2,26},{10... | collective-permute-start | bytes 393224 | tf_op jit(solution)/shard_map/ppermute | solution.py:217
